TPU v7x, 64 devices: a 2x2x8 block of a 4x4x8 slice. The times are simulated.
64 devices in a mesh: data: 4 (over x, y), stage: 16 (over z, core).
Axes of the slice: x: 2, y: 2, z: 8, core: 2. Of those that a mesh axis runs over, the one named last changes fastest.
The devices are a block of a 4x4x8 slice.
Arguments:
- x_init: float32 [4, 256, 16], P('data'), parts along dimension 0
- h_warm: bfloat16 [15, 4, 256, 768], P(None, 'data'), parts along dimension 1
- w_lat: bfloat16 [16, 16, 768], P('stage')
- w_qkv: bfloat16 [16, 768, 2304], P('stage')
- w_o: bfloat16 [16, 12, 64, 768], P('stage')
- w_up: bfloat16 [16, 768, 3072], P('stage')
- w_down: bfloat16 [16, 3072, 768], P('stage')
- w_out: bfloat16 [768, 16], replicated
- ada_mods: float32 [4, 16, 6, 768], P(None, 'stage')
- alpha_coef: float32 [4], replicated
- beta_coef: float32 [4], replicated
Outputs:
- output 1: float32 [4, 256, 16], P('data'), parts along dimension 0
- output 2: bfloat16 [16, 4, 256, 768], P('stage', 'data'), parts along dimension 1
There are 4 independent parts. A program takes and returns all parts, laid end to end along the dimension named above; an argument that names none is the same for every part.
All inputs are finite; a program needn't handle non-finite values.
Results may differ from a plain program's by a relative error of at most 0.0153327.
Values are sent between devices in bfloat16 or wider.
A program may use at most 768 MiB of HBM per device.

v0:
```python
import jax
import jax.numpy as jnp
from jax import lax
from jax.sharding import PartitionSpec as P


def layer_norm(h_cur):
    row_mean = jnp.mean(h_cur, axis=-1, keepdims=True)
    centered = h_cur - row_mean
    row_var = jnp.mean(centered * centered, axis=-1, keepdims=True)
    return centered * lax.rsqrt(row_var + 1e-6)


def value_a9(h_cur, w_qkv, w_o, w_up, w_down, mod_vec):
    batch_size, tokens = h_cur.shape[0], h_cur.shape[1]
    num_heads, head_dim = w_o.shape[0], w_o.shape[1]
    u_attn = (layer_norm(h_cur) * (1.0 + mod_vec[1]) + mod_vec[0]).astype(jnp.bfloat16)
    qkv_proj = jnp.einsum('bnd,de->bne', u_attn, w_qkv, preferred_element_type=jnp.float32).astype(jnp.bfloat16)
    qkv_proj = qkv_proj.reshape(batch_size, tokens, 3, num_heads, head_dim)
    scores = jnp.einsum('bqhd,bkhd->bhqk', qkv_proj[:, :, 0], qkv_proj[:, :, 1], preferred_element_type=jnp.float32) * head_dim ** -0.5
    attn_probs = jax.nn.softmax(scores, axis=-1).astype(jnp.bfloat16)
    attn_out = jnp.einsum('bhqk,bkhd->bqhd', attn_probs, qkv_proj[:, :, 2], preferred_element_type=jnp.float32).astype(jnp.bfloat16)
    h_cur = h_cur + mod_vec[2] * jnp.einsum('bqhd,hde->bqe', attn_out, w_o, preferred_element_type=jnp.float32)
    u_mlp = (layer_norm(h_cur) * (1.0 + mod_vec[4]) + mod_vec[3]).astype(jnp.bfloat16)
    hidden = jax.nn.gelu(jnp.einsum('bnd,df->bnf', u_mlp, w_up, preferred_element_type=jnp.float32), approximate=True).astype(jnp.bfloat16)
    return h_cur + mod_vec[5] * jnp.einsum('bnf,fd->bnd', hidden, w_down, preferred_element_type=jnp.float32)


def solution(mesh):
    stages = mesh.shape['stage']
    forward = [(dev_idx, dev_idx + 1) for dev_idx in range(stages - 1)]

    def stage_program(x_init, h_warm, w_lat, w_qkv, w_o, w_up, w_down, w_out, ada_mods, alpha_coef, beta_coef):
        stage_idx = lax.axis_index('stage')
        num_steps = ada_mods.shape[0]
        warm_in = lax.dynamic_index_in_dim(h_warm, jnp.maximum(stage_idx - 1, 0), axis=0, keepdims=False)
        stale_in = jnp.where(stage_idx > 0, warm_in, jnp.zeros_like(warm_in))
        x_cur = x_init
        for step_idx in range(num_steps):
            h_cur = stale_in.astype(jnp.float32) + jnp.einsum('bnc,cd->bnd', x_cur.astype(jnp.bfloat16), w_lat[0], preferred_element_type=jnp.float32)
            for layer_idx in range(w_qkv.shape[0]):
                h_cur = value_a9(h_cur, w_qkv[layer_idx], w_o[layer_idx], w_up[layer_idx], w_down[layer_idx], ada_mods[step_idx, layer_idx])
            stage_out = h_cur.astype(jnp.bfloat16)
            if step_idx < num_steps - 1:
                stale_in = lax.ppermute(stage_out, 'stage', perm=forward)
            eps_pred = jnp.einsum('bnd,dc->bnc', stage_out, w_out, preferred_element_type=jnp.float32)
            x_last = jnp.where(stage_idx == stages - 1, alpha_coef[step_idx] * x_cur + beta_coef[step_idx] * eps_pred, 0.0)
            x_cur = lax.psum(x_last, 'stage')
        return x_cur, stage_out[None]

    return jax.shard_map(stage_program, mesh=mesh,
                         in_specs=(P('data'), P(None, 'data'), P('stage'), P('stage'), P('stage'), P('stage'), P('stage'), P(), P(None, 'stage'), P(), P()),
                         out_specs=(P('data'), P('stage', 'data')), check_vma=False)
```

profile of v0, /device:TPU:125, one launch (start us, length us, event | category | flops | bytes accessed | tf_op | source)
XLA Modules:
  0.0 334.7 jit_solution(2637216451804643951)
XLA Ops:
  0.6 0.0 copy-start
  0.6 1.5 add_reduce_fusion
  2.2 1.7 slice_reduce_fusion.1
  3.9 1.4 fusion.287
  5.3 0.2 multiply_reduce_fusion.11
  5.5 0.6 copy-done.1
  6.2 2.2 convolution_convert_fusion.3
  8.3 2.4 copy.29
  10.7 1.7 fusion.198
  12.4 2.5 fusion.288
  14.9 4.8 %fusion.289 = (f32[256]{0:T(256)}, f32[256,768]{1,0:T(8,128)}) fusion(f32[256,768]{1,0:T(8,128)} %copy-done.1, bf16[1,12,64,768]{3,2,1,0:T(8,128)(2,1)} %param.15, f32[12,256,256]{1,2,0:T(8,128)} %get-tuple-element.37, f32[12,256]{1,0:T(8,128)S(1)} %get-tuple-element.36, bf16[1,256,3,12,64]{1,4,3,2,0:T(8,128)(2,1)} %bitcast.372, f32[768]{0:T(1024)} %get-tuple-element.24), kind=kOutput, calls=%fused_computation.305 | convolution fusion | flops 405012224 | bytes 6308864 | tf_op jit(solution)/shard_map/bqhd,hde->bqe/dot_general | solution.py:23
  19.7 0.6 broadcast_multiply_fusion.6
  20.3 1.4 multiply_reduce_fusion.10
  21.7 0.6 add_rsqrt_fusion.6
  22.2 8.1 %fusion.136 = bf16[256,768]{1,0:T(8,128)(2,1)} fusion(f32[256,768]{1,0:T(8,128)} %get-tuple-element.39, bf16[1,3072,768]{2,1,0:T(8,128)(2,1)} %param.17, bf16[1,768,3072]{2,1,0:T(8,128)(2,1)} %param.16, f32[768]{0:T(1024)} %get-tuple-element.18, f32[768]{0:T(1024)} %get-tuple-element.19, f32[256]{0:T(256)} %add_rsqrt_fusion.6, f32[256]{0:T(256)} %copy-done.7, ...), kind=kOutput, calls=%fused_computation.118 | convolution fusion | flops 2424569856 | bytes 10628096 | tf_op jit(solution)/shard_map/bnf,fd->bnd/dot_general | solution.py:26
  30.3 5.5 %collective-permute-start = (bf16[1,256,768]{2,1,0:T(8,128)(2,1)}, bf16[1,256,768]{2,1,0:T(8,128)(2,1)}, u32[]{:S(2)}, u32[]{:S(2)}) collective-permute-start(bf16[1,256,768]{2,1,0:T(8,128)(2,1)} %bitcast.373), channel_id=1, source_target_pairs={{0,1},{1,2},{2,3},{3,4},{4,5},{5,6},{6,7},{7,8},{8,9},{9,10},{10,1... | collective-permute-start | bytes 1179656 | tf_op jit(solution)/shard_map/ppermute | solution.py:45
  35.8 1.5 fusion.285
  37.3 1.5 fusion.286
  38.7 3.1 fusion.171
  41.8 45.7 %psum.28 = f32[1,256,16]{1,2,0:T(8,128)S(1)} all-reduce(f32[1,256,16]{1,2,0:T(8,128)} %fusion.171), channel_id=1, replica_groups=mesh['data'=4,'stage'=16] {'stage'}, use_global_device_ids=true, to_apply=%region_6.7 | all-reduce | flops 4096 | bytes 32768 | tf_op jit(solution)/shard_map/psum | solution.py:48
  87.6 1.4 fusion.250
  89.0 1.5 multiply_reduce_fusion.9
  90.5 3.2 convolution_convert_fusion.2
  93.8 2.4 copy.31
  96.1 1.7 fusion.197
  97.9 3.1 fusion.290
  100.9 4.9 %fusion.291 = (f32[256]{0:T(256)}, f32[1,256,768]{2,1,0:T(8,128)}) fusion(bf16[1,12,64,768]{3,2,1,0:T(8,128)(2,1)} %param.15, f32[12,256,256]{1,2,0:T(8,128)} %get-tuple-element.43, f32[12,256]{1,0:T(8,128)} %get-tuple-element.42, bf16[1,256,3,12,64]{1,4,3,2,0:T(8,128)(2,1)} %bitcast.366, f32[768]{0:T(1024)} %get-tuple-element.17, ...), kind=kOutput, calls=%fused_computation.307 | convolution fusion | flops 405405440 | bytes 6706176 | tf_op jit(solution)/shard_map/bqhd,hde->bqe/dot_general | solution.py:23
  105.8 0.7 broadcast_multiply_fusion.4
  106.5 0.6 copy-done.8
  107.1 1.4 multiply_reduce_fusion.8
  108.5 0.6 add_rsqrt_fusion.4
  109.0 8.0 %fusion.139 = bf16[1,256,768]{2,1,0:T(8,128)(2,1)} fusion(f32[1,256,768]{2,1,0:T(8,128)} %get-tuple-element.45, bf16[1,3072,768]{2,1,0:T(8,128)(2,1)} %param.17, bf16[1,768,3072]{2,1,0:T(8,128)(2,1)} %param.16, f32[768]{0:T(1024)} %get-tuple-element.12, f32[768]{0:T(1024)} %get-tuple-element.13, f32[256]{0:T(256)} %add_rsqrt_fusion.4, f32[256]{0:T(256)} %copy-done.8, ...), kind=kOutput, calls=%fused_computation.119 | convolution fusion | flops 2424569856 | bytes 10628096 | tf_op jit(solution)/shard_map/bnf,fd->bnd/dot_general | solution.py:26
  117.1 5.4 %collective-permute-start.1 = (bf16[1,256,768]{2,1,0:T(8,128)(2,1)}, bf16[1,256,768]{2,1,0:T(8,128)(2,1)}, u32[]{:S(2)}, u32[]{:S(2)}) collective-permute-start(bf16[1,256,768]{2,1,0:T(8,128)(2,1)} %fusion.139), channel_id=1, source_target_pairs={{0,1},{1,2},{2,3},{3,4},{4,5},{5,6},{6,7},{7,8},{8,9},{9,10},{10,1... | collective-permute-start | bytes 1179656 | tf_op jit(solution)/shard_map/ppermute | solution.py:45
  122.5 3.1 fusion.168
  125.6 45.7 %psum.29 = f32[1,256,16]{1,2,0:T(8,128)S(1)} all-reduce(f32[1,256,16]{1,2,0:T(8,128)} %fusion.168), channel_id=1, replica_groups=mesh['data'=4,'stage'=16] {'stage'}, use_global_device_ids=true, to_apply=%region_13.14 | all-reduce | flops 4096 | bytes 32768 | tf_op jit(solution)/shard_map/psum | solution.py:48
  171.4 1.4 fusion.251
  172.8 1.5 multiply_reduce_fusion.7
  174.3 3.2 convolution_convert_fusion.1
  177.6 2.4 copy.33
  179.9 1.7 fusion.196
  181.7 3.1 fusion.292
  184.7 4.9 %fusion.293 = (f32[256]{0:T(256)}, f32[1,256,768]{2,1,0:T(8,128)}) fusion(bf16[1,12,64,768]{3,2,1,0:T(8,128)(2,1)} %param.15, f32[12,256,256]{1,2,0:T(8,128)} %get-tuple-element.49, f32[12,256]{1,0:T(8,128)} %get-tuple-element.48, bf16[1,256,3,12,64]{1,4,3,2,0:T(8,128)(2,1)} %bitcast.368, f32[768]{0:T(1024)} %get-tuple-element.11, ...), kind=kOutput, calls=%fused_computation.309 | convolution fusion | flops 405405440 | bytes 6706176 | tf_op jit(solution)/shard_map/bqhd,hde->bqe/dot_general | solution.py:23
  189.6 0.7 broadcast_multiply_fusion.2
  190.3 0.6 copy-done.9
  190.9 1.4 multiply_reduce_fusion.6
  192.3 0.6 add_rsqrt_fusion.2
  192.8 8.1 %fusion.142 = bf16[1,256,768]{2,1,0:T(8,128)(2,1)} fusion(f32[1,256,768]{2,1,0:T(8,128)} %get-tuple-element.51, bf16[1,3072,768]{2,1,0:T(8,128)(2,1)} %param.17, bf16[1,768,3072]{2,1,0:T(8,128)(2,1)} %param.16, f32[768]{0:T(1024)} %get-tuple-element.6, f32[768]{0:T(1024)} %get-tuple-element.7, f32[256]{0:T(256)} %add_rsqrt_fusion.2, f32[256]{0:T(256)} %copy-done.9, ...), kind=kOutput, calls=%fused_computation.120 | convolution fusion | flops 2424569856 | bytes 10628096 | tf_op jit(solution)/shard_map/bnf,fd->bnd/dot_general | solution.py:26
  200.9 5.4 %collective-permute-start.2 = (bf16[1,256,768]{2,1,0:T(8,128)(2,1)}, bf16[1,256,768]{2,1,0:T(8,128)(2,1)}, u32[]{:S(2)}, u32[]{:S(2)}) collective-permute-start(bf16[1,256,768]{2,1,0:T(8,128)(2,1)} %fusion.142), channel_id=1, source_target_pairs={{0,1},{1,2},{2,3},{3,4},{4,5},{5,6},{6,7},{7,8},{8,9},{9,10},{10,1... | collective-permute-start | bytes 1179656 | tf_op jit(solution)/shard_map/ppermute | solution.py:45
  206.3 3.1 fusion.165
  209.4 45.7 %psum.30 = f32[1,256,16]{1,2,0:T(8,128)S(1)} all-reduce(f32[1,256,16]{1,2,0:T(8,128)} %fusion.165), channel_id=1, replica_groups=mesh['data'=4,'stage'=16] {'stage'}, use_global_device_ids=true, to_apply=%region_20.21 | all-reduce | flops 4096 | bytes 32768 | tf_op jit(solution)/shard_map/psum | solution.py:48
  255.2 1.4 fusion.252
  256.6 1.5 multiply_reduce_fusion.5
  258.1 3.2 convolution_convert_fusion
  261.4 2.4 copy.35
  263.7 1.7 fusion.195
  265.5 3.1 fusion.294
  268.5 4.9 %fusion.295 = (f32[256]{0:T(256)}, f32[1,256,768]{2,1,0:T(8,128)}) fusion(bf16[1,12,64,768]{3,2,1,0:T(8,128)(2,1)} %param.15, f32[12,256,256]{1,2,0:T(8,128)} %get-tuple-element.55, f32[12,256]{1,0:T(8,128)} %get-tuple-element.54, bf16[1,256,3,12,64]{1,4,3,2,0:T(8,128)(2,1)} %bitcast.370, f32[768]{0:T(1024)} %get-tuple-element.5, ...), kind=kOutput, calls=%fused_computation.311 | convolution fusion | flops 405405440 | bytes 6706176 | tf_op jit(solution)/shard_map/bqhd,hde->bqe/dot_general | solution.py:23
  273.4 0.7 broadcast_multiply_fusion
  274.1 0.6 copy-done.6
  274.7 1.4 multiply_reduce_fusion.4
  276.1 0.6 add_rsqrt_fusion
  276.7 8.1 %fusion.145 = bf16[1,256,768]{2,1,0:T(8,128)(2,1)} fusion(f32[1,256,768]{2,1,0:T(8,128)} %get-tuple-element.57, bf16[1,3072,768]{2,1,0:T(8,128)(2,1)} %param.17, bf16[1,768,3072]{2,1,0:T(8,128)(2,1)} %param.16, f32[768]{0:T(1024)} %get-tuple-element.25, f32[768]{0:T(1024)} %get-tuple-element.21, f32[256]{0:T(256)} %add_rsqrt_fusion, f32[256]{0:T(256)} %copy-done.6, ...), kind=kOutput, calls=%fused_computation.121 | convolution fusion | flops 2424569856 | bytes 10628096 | tf_op jit(solution)/shard_map/bnf,fd->bnd/dot_general | solution.py:26
  284.7 3.1 fusion.162
  287.8 46.9 %psum.31 = f32[1,256,16]{1,2,0:T(8,128)} all-reduce(f32[1,256,16]{1,2,0:T(8,128)} %fusion.162), channel_id=1, replica_groups=mesh['data'=4,'stage'=16] {'stage'}, use_global_device_ids=true, to_apply=%region_27.28 | all-reduce | flops 4096 | bytes 32768 | tf_op jit(solution)/shard_map/psum | solution.py:48
  (26 shorter events, 0.1 us)
Async XLA Ops:
  0.6 5.5 %copy-start = (bf16[1,768,2304]{2,1,0:T(8,128)(2,1)S(1)}, bf16[1,768,2304]{2,1,0:T(8,128)(2,1)}, u32[]{:S(2)}) copy-start(bf16[1,768,2304]{2,1,0:T(8,128)(2,1)} %param.14) | copy-start | bytes 10616836
  5.3 0.9 copy-start.1
  20.3 1.9 copy-start.7
  22.2 16.5 %copy-start.5 = (f32[1,256,16]{1,2,0:T(8,128)S(1)}, f32[1,256,16]{1,2,0:T(8,128)}, u32[]{:S(2)}) copy-start(f32[1,256,16]{1,2,0:T(8,128)} %param.11) | copy-start | bytes 49156
  30.3 57.3 %collective-permute-start = (bf16[1,256,768]{2,1,0:T(8,128)(2,1)}, bf16[1,256,768]{2,1,0:T(8,128)(2,1)}, u32[]{:S(2)}, u32[]{:S(2)}) collective-permute-start(bf16[1,256,768]{2,1,0:T(8,128)(2,1)} %bitcast.373), channel_id=1, source_target_pairs={{0,1},{1,2},{2,3},{3,4},{4,5},{5,6},{6,7},{7,8},{8,9},{9,10},{10,1... | collective-permute-start | bytes 1179656 | tf_op jit(solution)/shard_map/ppermute | solution.py:45
  89.0 1.6 copy-start.2
  106.5 0.6 copy-start.8
  117.1 54.3 %collective-permute-start.1 = (bf16[1,256,768]{2,1,0:T(8,128)(2,1)}, bf16[1,256,768]{2,1,0:T(8,128)(2,1)}, u32[]{:S(2)}, u32[]{:S(2)}) collective-permute-start(bf16[1,256,768]{2,1,0:T(8,128)(2,1)} %fusion.139), channel_id=1, source_target_pairs={{0,1},{1,2},{2,3},{3,4},{4,5},{5,6},{6,7},{7,8},{8,9},{9,10},{10,1... | collective-permute-start | bytes 1179656 | tf_op jit(solution)/shard_map/ppermute | solution.py:45
  172.7 1.6 copy-start.3
  190.3 0.6 copy-start.9
  200.9 54.3 %collective-permute-start.2 = (bf16[1,256,768]{2,1,0:T(8,128)(2,1)}, bf16[1,256,768]{2,1,0:T(8,128)(2,1)}, u32[]{:S(2)}, u32[]{:S(2)}) collective-permute-start(bf16[1,256,768]{2,1,0:T(8,128)(2,1)} %fusion.142), channel_id=1, source_target_pairs={{0,1},{1,2},{2,3},{3,4},{4,5},{5,6},{6,7},{7,8},{8,9},{9,10},{10,1... | collective-permute-start | bytes 1179656 | tf_op jit(solution)/shard_map/ppermute | solution.py:45
  256.6 1.6 copy-start.4
  274.1 0.6 copy-start.6
where the time goes:
time: 336 us; the launch traced here: 335 us
  blocking collectives  184 us (55%)
  matrix products  88.4 us (26%)
  other arithmetic  30.1 us (9%)
  starting transfers between devices  16.3 us (5%)
  local copies, waits for them, and re-layouts  14.8 us (4%)
    psum x4, blocking collectives, stage_program(): x_cur = lax.psum(x_last, 'stage')  184 us
    dot_general x4, matrix products, value_a9(): jnp.einsum('bnf,fd->bnd', hidden, w_down, preferred_element_type=jnp.floa...  32.2 us
    dot_general x4, matrix products, value_a9(): jnp.einsum('bqhd,hde->bqe', attn_out, w_o, preferred_element_type=jnp.flo...  19.5 us
    ppermute x3, starting transfers between devices, stage_program(): stale_in = lax.ppermute(stage_out, 'stage', perm=forward)  16.3 us
    dot_general x4, matrix products, stage_program(): jnp.einsum('bnd,dc->bnc', stage_out, w_out, preferred_element_type=jnp.fl...  12.4 us
    dot_general x4, matrix products, value_a9(): jnp.einsum('bnd,de->bne', u_attn, w_qkv, preferred_element_type=jnp.float32)  11.9 us
    sub x4, other arithmetic, value_a9(): attn_probs = jax.nn.softmax(scores, axis=-1).astype(jnp.bfloat16)  11.7 us
    reduce_sum x8, other arithmetic, layer_norm(): row_var = jnp.mean(centered * centered, axis=-1, keepdims=True)  10.2 us
  transfers between devices with their start and end apart: 3, of which 0 were waited for; matrix products, arithmetic and copies ran while one was open for 4% of the time, Pallas kernels for 0%

commit v1 on v0

v1 whole, which is shorter than its diff:
```python
import functools
import math

import jax
import jax.numpy as jnp
from jax import lax
from jax.experimental import pallas as pl
from jax.experimental.pallas import tpu as pltpu
from jax.sharding import PartitionSpec as P

MESH = pl.DeviceIdType.MESH
F32, BF16 = jnp.float32, jnp.bfloat16
LANES = 128
TILE = 256
EXP2_SCALE = math.log2(math.e)
GELU_A = math.sqrt(2.0 / math.pi)
GELU_B = GELU_A * 0.044715


def normed(h_rows, scale_row, shift_row):
    width = h_rows.shape[-1]
    centered = h_rows - jnp.sum(h_rows, axis=-1, keepdims=True) * (1.0 / width)
    row_var = jnp.sum(centered * centered, axis=-1, keepdims=True) * (1.0 / width)
    return (centered * lax.rsqrt(row_var + 1e-6) * (1.0 + scale_row) + shift_row).astype(BF16)


def gelu(val):
    half = 0.5 * val
    return half * jnp.tanh(val * (GELU_B * (val * val) + GELU_A)) + half


def dot(lhs, rhs):
    return jnp.dot(lhs, rhs, preferred_element_type=F32)


def dot_t(lhs, rhs):
    return lax.dot_general(lhs, rhs, (((1,), (1,)), ((), ())), preferred_element_type=F32)


def kernel(stages, head_dim, x_hbm, warm_hbm, lat_hbm, qkv_hbm, o_hbm, up_hbm, down_hbm, out_hbm, ada_hbm, alpha_ref, beta_ref,
           xo_ref, last_hbm,
           x_f, x_b, b_in, s_out, h_ref, u_ref, qkv_ref, p_ref, v_ref, a_ref, hid_ref, x_fin,
           w_lat, w_qkv, w_o, w_up, w_down, w_out, ada,
           load_sem, b_send, b_recv, x_send, x_recv, last_sem):
    steps = alpha_ref.shape[0]
    tokens, width = h_ref.shape
    me = lax.axis_index('stage')
    is_last = me == stages - 1

    def peer(idx):
        return {'stage': idx}

    loads = {}
    for idx, (name, src, dst) in enumerate((
            ('warm', warm_hbm.at[jnp.maximum(me - 1, 0), 0], b_in.at[0]),
            ('x', x_hbm.at[0], x_f),
            ('lat', lat_hbm.at[0], w_lat),
            ('ada', ada_hbm, ada),
            ('qkv', qkv_hbm.at[0], w_qkv),
            ('o', o_hbm.at[0], w_o),
            ('up', up_hbm.at[0], w_up),
            ('down', down_hbm.at[0], w_down),
            ('out', out_hbm, w_out))):
        loads[name] = pltpu.make_async_copy(src, dst, load_sem.at[idx])
        loads[name].start()

    barrier = pltpu.get_barrier_semaphore()

    def greet(idx):
        pl.semaphore_signal(barrier, inc=1, device_id=peer(idx), device_id_type=MESH)

    @pl.when(is_last)
    def _():
        for idx in range(stages - 1):
            greet(idx)

    @pl.when(jnp.logical_not(is_last))
    def _():
        greet(stages - 1)

        @pl.when(me > 0)
        def _():
            greet(me - 1)

        @pl.when(me < stages - 2)
        def _():
            greet(me + 1)

    def send_b(step):
        return pltpu.make_async_remote_copy(s_out.at[step], b_in.at[step + 1], b_send.at[step], b_recv.at[step],
                                            device_id=peer(me + 1), device_id_type=MESH)

    def send_x(step, idx):
        return pltpu.make_async_remote_copy(x_b.at[step + 1], x_b.at[step + 1], x_send.at[idx], x_recv.at[step],
                                            device_id=peer(idx), device_id_type=MESH)

    def send_final(idx):
        return pltpu.make_async_remote_copy(x_fin, x_fin, x_send.at[idx], x_recv.at[steps - 1],
                                            device_id=peer(idx), device_id_type=MESH)

    loads['warm'].wait()

    @pl.when(me == 0)
    def _():
        for step in range(steps):
            b_in[step] = jnp.zeros((tokens, width), BF16)

    loads['x'].wait()
    loads['lat'].wait()
    loads['ada'].wait()
    x_b[0] = x_f[...].astype(BF16)

    def one_step(step, carry):
        @pl.when(jnp.logical_and(step > 0, jnp.logical_not(is_last)))
        def _():
            send_x(step - 1, 0).wait_recv()

        @pl.when(jnp.logical_and(step > 0, me > 0))
        def _():
            send_b(step - 1).wait_recv()

        def row(kind):
            return ada[step, kind]

        for r in range(0, tokens, 64):
            h_rows = b_in[step, r:r + 64, :].astype(F32) + lax.dot_general(
                x_b[step, :, r:r + 64], w_lat[...], (((0,), (0,)), ((), ())), preferred_element_type=F32)
            h_ref[r:r + 64, :] = h_rows
            u_ref[r:r + 64, :] = normed(h_rows, row(1), row(0))

        @pl.when(step == 0)
        def _():
            loads['qkv'].wait()

        for col in range(0, 3 * width, TILE):
            qkv_ref[:, col:col + TILE] = dot(u_ref[...], w_qkv[:, col:col + TILE]).astype(BF16)

        per_group = TILE // head_dim
        lane_head = lax.broadcasted_iota(jnp.int32, (1, TILE), 1) // head_dim
        for col in range(0, width, TILE):
            keys = qkv_ref[:, width + col:width + col + TILE]
            for j in range(per_group):
                mine = lane_head == j
                v_ref[j * tokens:(j + 1) * tokens, :] = jnp.where(
                    mine, qkv_ref[:, 2 * width + col:2 * width + col + TILE], 0.0).astype(BF16)
                query = jnp.where(mine, qkv_ref[:, col:col + TILE], 0.0).astype(BF16)
                scores = dot_t(query, keys)
                top = jnp.max(scores, axis=-1, keepdims=True)
                expd = jnp.exp2((scores - top) * (EXP2_SCALE * head_dim ** -0.5))
                total = jnp.sum(expd, axis=-1, keepdims=True)
                p_ref[:, j * tokens:(j + 1) * tokens] = (expd * (1.0 / total)).astype(BF16)
            a_ref[:, col:col + TILE] = dot(p_ref[...], v_ref[...]).astype(BF16)

        @pl.when(step == 0)
        def _():
            loads['o'].wait()

        for col in range(0, width, TILE):
            cols = slice(col, col + TILE)
            h_ref[:, cols] += row(2)[:, cols] * dot(a_ref[...], w_o[:, cols])
        for r in range(0, tokens, 64):
            u_ref[r:r + 64, :] = normed(h_ref[r:r + 64, :], row(4), row(3))

        @pl.when(step == 0)
        def _():
            loads['up'].wait()

        for col in range(0, w_up.shape[1], TILE):
            hid_ref[:, col:col + TILE] = gelu(dot(u_ref[...], w_up[:, col:col + TILE])).astype(BF16)

        @pl.when(step == 0)
        def _():
            loads['down'].wait()
            loads['out'].wait()

        for col in range(0, width, TILE):
            cols = slice(col, col + TILE)
            s_out[step, :, cols] = (h_ref[:, cols] + row(5)[:, cols] * dot(hid_ref[...], w_down[:, cols])).astype(BF16)

        @pl.when(step == 0)
        def _():
            pl.semaphore_wait(barrier, jnp.where(is_last, stages - 1, jnp.where(me == 0, 2, jnp.where(me == stages - 2, 2, 3))))

        @pl.when(jnp.logical_and(step < steps - 1, jnp.logical_not(is_last)))
        def _():
            send_b(step).start()

        @pl.when(is_last)
        def _():
            @pl.when(step > 0)
            def _():
                for idx in range(stages - 1):
                    send_x(step - 1, idx).wait_send()

            x_new = alpha_ref[step] * x_f[...] + beta_ref[step] * dot_t(w_out[...], s_out[step])
            x_f[...] = x_new

            @pl.when(step < steps - 1)
            def _():
                x_b[step + 1] = x_new.astype(BF16)
                for idx in range(stages - 1):
                    send_x(step, idx).start()

            @pl.when(step == steps - 1)
            def _():
                x_fin[...] = x_new
                for idx in range(stages - 1):
                    send_final(idx).start()

        return carry

    lax.fori_loop(0, steps, one_step, 0)

    put = pltpu.make_async_copy(s_out.at[steps - 1], last_hbm.at[0, 0], last_sem)
    put.start()

    @pl.when(jnp.logical_not(is_last))
    def _():
        for step in range(steps - 1):
            send_b(step).wait_send()
        send_final(0).wait_recv()

    @pl.when(is_last)
    def _():
        for idx in range(stages - 1):
            send_final(idx).wait_send()

    xo_ref[0] = x_fin[...]
    put.wait()


def solution(mesh):
    stages = mesh.shape['stage']

    def stage_program(x_init, h_warm, w_lat, w_qkv, w_o, w_up, w_down, w_out, ada_mods, alpha_coef, beta_coef):
        _, tokens, chans = x_init.shape
        width = h_warm.shape[-1]
        hidden = w_up.shape[-1]
        steps = ada_mods.shape[0]
        inner = w_o.shape[1] * w_o.shape[2]
        x_t = jnp.swapaxes(x_init, 1, 2)
        o_flat = w_o.reshape(w_o.shape[0], inner, width)
        ada = jnp.swapaxes(ada_mods, 1, 2)
        anywhere = pl.BlockSpec(memory_space=pl.ANY)
        scalars = pl.BlockSpec(memory_space=pltpu.SMEM)
        vmem = pltpu.VMEM
        dma = pltpu.SemaphoreType.DMA
        x_out, last = pl.pallas_call(
            functools.partial(kernel, stages, w_o.shape[2]),
            out_shape=(jax.ShapeDtypeStruct((1, chans, tokens), F32),
                       jax.ShapeDtypeStruct((1, 1, tokens, width), BF16)),
            in_specs=[anywhere] * 9 + [scalars] * 2,
            out_specs=(pl.BlockSpec(memory_space=vmem), anywhere),
            scratch_shapes=[
                vmem((chans, tokens), F32),
                vmem((steps, chans, tokens), BF16),
                vmem((steps, tokens, width), BF16),
                vmem((steps, tokens, width), BF16),
                vmem((tokens, width), F32),
                vmem((tokens, width), BF16),
                vmem((tokens, 3 * width), BF16),
                vmem((tokens, 4 * tokens), BF16),
                vmem((4 * tokens, TILE), BF16),
                vmem((tokens, width), BF16),
                vmem((tokens, hidden), BF16),
                vmem((chans, tokens), F32),
                vmem(w_lat.shape[1:], BF16),
                vmem(w_qkv.shape[1:], BF16),
                vmem((inner, width), BF16),
                vmem(w_up.shape[1:], BF16),
                vmem(w_down.shape[1:], BF16),
                vmem((chans, width), BF16),
                vmem(ada.shape, F32),
                dma((9,)),
                dma((steps,)),
                dma((steps,)),
                dma((stages,)),
                dma((steps,)),
                dma,
            ],
            compiler_params=pltpu.CompilerParams(collective_id=0, has_side_effects=True, vmem_limit_bytes=60 << 20),
        )(x_t, h_warm, w_lat, w_qkv, o_flat, w_up, w_down, w_out.T, ada, alpha_coef, beta_coef)
        return jnp.swapaxes(x_out, 1, 2), last

    return jax.shard_map(stage_program, mesh=mesh,
                         in_specs=(P('data'), P(None, 'data'), P('stage'), P('stage'), P('stage'), P('stage'), P('stage'), P(), P(None, 'stage'), P(), P()),
                         out_specs=(P('data'), P('stage', 'data')), check_vma=False)
```

time: 336 us -> 60.3 us (0.18)
  the two profiles are of different devices: /device:TPU:125 before, /device:TPU:21 now
where the time goes in v1:
time: 60.3 us; the launch traced here: 60.1 us
  Pallas kernels  56.4 us (94%)
  local copies, waits for them, and re-layouts  3.09 us (5%)
  between operations  0.64 us (1%)
    pallas_call x1, Pallas kernels, stage_program(): pl.pallas_call(functools.partial(kernel, stages, w_o.shape[2]), out_shape...  56.4 us
    unnamed x2, local copies, waits for them, and re-layouts  3.09 us

profile of v1, /device:TPU:21, one launch (start us, length us, event | category | flops | bytes accessed | tf_op | source)
XLA Modules:
  0.0 60.1 jit_solution(13710947821610888347)
XLA Ops:
  0.6 56.4 %shard_map.122 = (f32[1,16,256]{2,1,0:T(8,128)}, bf16[1,1,256,768]{3,2,1,0:T(8,128)(2,1)}) custom-call(f32[1,16,256]{2,1,0:T(8,128)} %bitcast.8, bf16[15,1,256,768]{3,2,1,0:T(8,128)(2,1)} %warm_hbm.1, bf16[1,16,768]{2,1,0:T(8,128)(2,1)} %lat_hbm.1, bf16[1,768,2304]{2,1,0:T(8,128)(2,1)} %qkv_hbm.1, bf16[1,768,768]{2,1,0:T(8,128)(2,1)} %bitcast.5, ...), custom_call_target="tpu_custom_call" | custom-call | tf_op jit(solution)/shard_map/pallas_call | solution.py:248
  57.1 1.3 %copy.15 = f32[1,256,16]{1,2,0:T(8,128)} copy(f32[1,256,16]{1,2,0:T(8,128)} %bitcast.9) | data formatting | bytes 32768
  58.4 1.8 %copy.16 = bf16[1,1,256,768]{3,2,1,0:T(8,128)(2,1)} copy(bf16[1,1,256,768]{3,2,1,0:T(8,128)(2,1)} %get-tuple-element.9) | data formatting | bytes 786432
